TPU v7x, 256 devices: a whole 4x4x8 slice. The times are simulated.
256 devices in a mesh: lon: 16 (over x_lo, z), lat: 16 (over x_hi, y, core).
Axes of the slice: x: 4 (x_hi: 2, x_lo: 2; x = x_hi * 2 + x_lo), y: 4, z: 8, core: 2. Of those that a mesh axis runs over, the one named last changes fastest.
Arguments:
- grid_field: float32 [4, 256, 16, 2048], P(None, 'lat', None, 'lon'), may hold values from -6 to 6
- lat_weight: float32 [256], replicated, may hold values from 0.3 to 3
Outputs:
- spec_real: float32 [4, 256, 16, 1024], P(None, None, 'lat', 'lon')
- spec_imag: float32 [4, 256, 16, 1024], P(None, None, 'lat', 'lon')
All inputs are finite; a program needn't handle non-finite values.
Results may differ from a plain program's by a relative error of at most 0.000071.
Values sent between devices are 32-bit elements; how exact they have to be, the bound alone decides.
No kernel may reach another device: no remote copies, remote signals or barrier semaphores. Data moves between devices by JAX's collectives and lax.ppermute only.
A program may use at most 64 MiB of HBM per device.

v0:
```python
import math

import jax
import jax.numpy as jnp
from jax import lax
from jax.sharding import PartitionSpec as P

MODES = 1024


two_pi = 2.0 * math.pi


def mode_table(lon_ids, mode_ids, length):
    phases = lon_ids[:, None] * mode_ids[None, :] % length
    angles = phases.astype(jnp.float32) * (two_pi / length)
    normalizer = 1.0 / math.sqrt(length)
    return (jnp.cos(angles) * normalizer, -jnp.sin(angles) * normalizer)


def slot_table(lon_ids, slot_ids, mode_dev, length):
    mode_ids = slot_ids // (2 * mode_dev) * mode_dev + slot_ids % mode_dev
    is_imag = slot_ids // mode_dev % 2 == 1
    cosine, sine_part = mode_table(lon_ids, mode_ids, length)
    return jnp.where(is_imag[None, :], sine_part, cosine)


def per_device(grid_field, lat_weight):
    fields, lat_dev, radius_count, lon_dev = grid_field.shape
    cycle_size = lax.axis_size("lon")
    length = cycle_size * lon_dev
    mode_dev = MODES // cycle_size
    my_index = lax.axis_index("lon")
    row_count = fields * lat_dev * radius_count
    flat_grid = grid_field.reshape(row_count, lon_dev)
    lon_ids = my_index * lon_dev + jnp.arange(lon_dev, dtype=jnp.int32)
    slot_ids = jnp.arange(2 * mode_dev * lax.axis_size("lon"), dtype=jnp.int32)
    dft_table = slot_table(lon_ids, slot_ids, mode_dev, length)
    summed = lax.psum_scatter(
        lax.dot_general(
            dft_table,
            flat_grid,
            (((0,), (1,)), ((), ())),
            precision=lax.Precision.HIGHEST,
            preferred_element_type=jnp.float32,
        ),
        "lon",
        scatter_dimension=0,
        tiled=True,
    )
    spectra = summed.T.reshape(fields, lat_dev, radius_count, 2, mode_dev)
    gathered = lax.all_to_all(spectra, "lat", split_axis=2, concat_axis=1, tiled=True)
    weights_row = lat_weight[None, :, None, None]
    return (gathered[:, :, :, 0, :] * weights_row, gathered[:, :, :, 1, :] * weights_row)


def solution(mesh):
    in_specs = (P(None, "lat", None, "lon"), P())
    out_specs = (P(None, None, "lat", "lon"), P(None, None, "lat", "lon"))
    return jax.shard_map(
        per_device, mesh=mesh, in_specs=in_specs, out_specs=out_specs, check_vma=False
    )
```

profile of v0, /device:TPU:1, one launch (start us, length us, event | category | flops | bytes accessed | tf_op | source)
XLA Modules:
  0.0 160.1 jit_solution(15810153436678199506)
XLA Ops:
  7.2 0.0 copy-start
  7.2 0.0 reduce-scatter.2.cloned.1.call-start
  7.3 0.9 copy-done
  8.2 13.0 %fusion.3 = f32[2048,1024]{1,0:T(8,128)} fusion(f32[1024,128]{1,0:T(8,128)S(1)} %bitcast.23, s32[2048]{0:T(1024)S(1)} %fusion.34, s32[128]{0:T(128)S(1)} %iota_add_fusion, pred[2048]{0:T(1024)(128)(4,1)S(1)} %fusion.31), kind=kOutput, calls=%fused_computation.8 | convolution fusion | flops 3225944064 | bytes 8923648 | tf_op jit(solution)/shard_map/dot_general | solution.py:40
  21.2 0.0 reduce-scatter.2.cloned.1.call-update
  21.2 0.0 copy-start.1
  21.2 105.0 %reduce-scatter.2.cloned.1.call-done = f32[128,1024]{1,0:T(8,128)} async-done(((f32[2048,1024]{1,0:T(8,128)}), f32[128,1024]{1,0:T(8,128)}) %reduce-scatter.2.cloned.1.call-update) | async-done | bytes 524304 | tf_op jit(solution)/shard_map/reduce_scatter | solution.py:39
  126.3 1.2 copy.11
  127.5 0.6 reshape.87
  128.1 0.6 copy.19
  128.7 1.1 reshape.88
  129.8 18.1 %all_to_all.18 = f32[16,1,8192]{2,1,0:T(1,128)S(1)} all-to-all(f32[16,1,8192]{2,1,0:T(1,128)S(1)} %reshape.88), channel_id=1, replica_groups=mesh['lon'=16,'lat'=16] {'lat'}, dimensions={0} | all-to-all | bytes 1048576 | tf_op jit(solution)/shard_map/all_to_all | solution.py:52
  148.0 0.5 broadcast.154
  148.5 1.9 %reduce = f32[16,8192]{1,0:T(8,128)S(1)} reduce(f32[16,1,8192]{2,1,0:T(1,128)S(1)} %all_to_all.18, f32[]{:T(128)} %broadcast.154), dimensions={1}, to_apply=%all_to_all.13.reduce_sub_computation | reduce | bytes 1048580 | tf_op jit(solution)/shard_map/all_to_all | solution.py:52
  150.4 0.8 reshape.89
  151.1 0.1 bitcast_bitcast_fusion
  151.2 0.1 copy.13
  151.3 0.0 copy-done.1
  151.3 0.1 fusion.14
  151.5 0.9 copy.15
  152.4 0.9 copy.16
  (3 shorter events, 0.0 us)
Async XLA Ops:
  7.2 1.0 copy-start
  7.2 119.1 %reduce-scatter.2.cloned.1.call-start = ((), (), s32[]{:S(2)}) async-start(), calls=%async_computation.2 | async-start | bytes 8912896 | tf_op jit(solution)/shard_map/reduce_scatter | solution.py:39
  21.2 130.1 %copy-start.1 = (f32[256]{0:T(256)S(1)}, f32[256]{0:T(256)}, u32[]{:S(2)}) copy-start(f32[256]{0:T(256)} %param.3) | copy-start | bytes 3076
Sparse Core Ops, SparseCore 0:
  21.4 104.8 reduce-scatter.1
where the time goes:
time: 160 us
  waiting for transfers between devices  105 us (66%)
  blocking collectives  18.1 us (11%)
  between operations  14.1 us (9%)
  matrix products  13 us (8%)
  local copies, waits for them, and re-layouts  7.7 us (5%)
  other arithmetic  2.04 us (1%)
    reduce_scatter x1, waiting for transfers between devices, per_device(): lax.psum_scatter(lax.dot_general(dft_table, flat_grid, (((0,), (1,)), (()...  105 us
    all_to_all x1, blocking collectives, per_device(): lax.all_to_all(spectra, 'lat', split_axis=2, concat_axis=1, tiled=True)  18.1 us
    dot_general x1, matrix products, per_device(): lax.dot_general(dft_table, flat_grid, (((0,), (1,)), ((), ())), precision...  13 us
    unnamed x8, local copies, waits for them, and re-layouts  4.59 us
  transfers between devices with their start and end apart: 1, of which 1 were waited for; matrix products, arithmetic and copies ran while one was open for 0% of the time, Pallas kernels for 0%

commit v1 on v0

v1 whole, which is shorter than its diff:
```python
import functools
import math

import jax
import jax.numpy as jnp
import numpy as np
from jax import lax
from jax.experimental import pallas as pl
from jax.experimental.pallas import tpu as pltpu
from jax.sharding import PartitionSpec as P

LENGTH = 2048
PEERS = 16
BLOCK = 128
ROWS = 64


def mode_tables():
    b = np.arange(BLOCK)
    tables = np.zeros((8, 256, 256))
    for residue in range(PEERS):
        group, e = np.divmod(np.arange(128), 8)
        part, step = np.divmod(e, 4)
        owner = (group - residue) % PEERS
        mode = residue + PEERS * (4 * owner + step)
        phase = 2.0 * math.pi * (b[:, None] * mode[None, :] % LENGTH) / LENGTH
        cosine = np.cos(phase) / math.sqrt(LENGTH)
        sine = np.sin(phase) / math.sqrt(LENGTH)
        sign = -1.0 if residue > 8 else 1.0
        from_real = np.where(part == 0, cosine, -sine)
        from_imag = sign * np.where(part == 0, sine, cosine)
        if residue == 0:
            tables[0, :128, :128] = from_real
        elif residue == 8:
            tables[0, 128:, 128:] = from_real
        else:
            tile = min(residue, PEERS - residue)
            at = 0 if residue < 8 else 128
            tables[tile, :128, at : at + 128] = from_real
            tables[tile, 128:, at : at + 128] = from_imag
    table = tables.astype(np.float32)
    high = table.astype(jnp.bfloat16)
    low = (table - high.astype(np.float32)).astype(jnp.bfloat16)
    return np.stack([high, low])


def real_dft16(x):
    h = math.sqrt(0.5)
    c1, c3 = math.cos(math.pi / 8), math.cos(3 * math.pi / 8)
    s1, s3 = math.sin(math.pi / 8), math.sin(3 * math.pi / 8)
    s = [x[a] + x[a + 8] for a in range(8)]
    d = [x[a] - x[a + 8] for a in range(8)]
    p = [s[a] + s[a + 4] for a in range(4)]
    q = [s[a] - s[a + 4] for a in range(4)]
    out = [None] * 9
    even, odd = p[0] + p[2], p[1] + p[3]
    out[0] = (even + odd, None)
    out[8] = (even - odd, None)
    out[4] = (p[0] - p[2], p[3] - p[1])
    diff, total = h * (q[1] - q[3]), h * (q[1] + q[3])
    out[2] = (q[0] + diff, -q[2] - total)
    out[6] = (q[0] - diff, q[2] - total)
    e1, e2, e3 = d[1] - d[7], h * (d[2] - d[6]), d[3] - d[5]
    g1, g2, g3 = d[1] + d[7], h * (d[2] + d[6]), d[3] + d[5]
    r1, r3 = d[0] + e2, d[0] - e2
    u1, u3 = c1 * e1 + c3 * e3, c3 * e1 - c1 * e3
    i1, i3 = g2 + d[4], g2 - d[4]
    v1, v3 = s1 * g1 + s3 * g3, s3 * g1 - s1 * g3
    out[1] = (r1 + u1, -(v1 + i1))
    out[7] = (r1 - u1, i1 - v1)
    out[3] = (r3 + u3, -(v3 + i3))
    out[5] = (r3 - u3, i3 - v3)
    return out


def transform_kernel(y_ref, table_ref, o_ref, lhs, mid):
    for g in range(ROWS // 16):
        rows = slice(16 * g, 16 * g + 16)
        dft = real_dft16([y_ref[a, rows, :] for a in range(PEERS)])
        for tile in range(8):
            pair = (dft[0][0], dft[8][0]) if tile == 0 else dft[tile]
            for part in range(2):
                high = pair[part].astype(jnp.bfloat16)
                low = (pair[part] - high.astype(jnp.float32)).astype(jnp.bfloat16)
                at = slice(128 * part, 128 * part + 128)
                lhs[tile, 16 * g : 16 * g + 16, at] = high
                lhs[tile, ROWS + 16 * g : ROWS + 16 * g + 16, at] = low
    dot = functools.partial(jnp.dot, preferred_element_type=jnp.float32)
    for tile in range(8):
        both = dot(lhs[tile], table_ref[0, tile])
        total = both[:ROWS] + both[ROWS:] + dot(lhs[tile, :ROWS, :], table_ref[1, tile])
        mid[tile] = total[:, :128]
        mid[8 if tile == 0 else PEERS - tile] = total[:, 128:]
    group = lax.broadcasted_iota(jnp.int32, (8, 128), 1) // 8
    bits = [(group >> s) % 2 == 1 for s in range(4)]
    for g in range(ROWS // 8):
        v = [mid[k, 8 * g : 8 * g + 8, :] for k in range(PEERS)]
        for s in range(4):
            v = [jnp.where(bits[s], v[(i + (1 << s)) % PEERS], v[i]) for i in range(PEERS)]
        latitude, radius = g // 2, 8 * (g % 2)
        for j in range(PEERS):
            value = v[-j % PEERS]
            if j:
                value = pltpu.roll(value, 128 - 8 * j, 1)
            o_ref[pl.ds(radius * 64 + j * 4 + latitude, 8, stride=64), :] = value


def transform(y):
    return pl.pallas_call(
        transform_kernel,
        out_shape=jax.ShapeDtypeStruct((1024, 128), jnp.float32),
        in_specs=[pl.BlockSpec(memory_space=pltpu.VMEM)] * 2,
        out_specs=pl.BlockSpec(memory_space=pltpu.VMEM),
        scratch_shapes=[
            pltpu.VMEM((8, 2 * ROWS, 256), jnp.bfloat16),
            pltpu.VMEM((PEERS, ROWS, 128), jnp.float32),
        ],
        compiler_params=pltpu.CompilerParams(vmem_limit_bytes=16 << 20),
        cost_estimate=pl.CostEstimate(flops=2 * 8 * 192 * 256 * 256, bytes_accessed=3 << 20, transcendentals=0),
        name="transform",
    )(y, jnp.asarray(mode_tables()))


def weigh_kernel(g_ref, w_ref, re_ref, im_ref, turned):
    weights = w_ref[...]
    for f in range(4):
        rows = jnp.concatenate([g_ref[64 * i + 16 * f : 64 * i + 16 * f + 16, :] for i in range(16)], axis=0)
        for half in range(2):
            turned[half] = rows[128 * half : 128 * half + 128].T * weights[:, 128 * half : 128 * half + 128]
        for half in range(2):
            at = slice(128 * half, 128 * half + 128)
            for step in range(4):
                re_ref[f, 16 * step : 16 * step + 16, at] = turned[half, pl.ds(step, 16, stride=8), :]
                im_ref[f, 16 * step : 16 * step + 16, at] = turned[half, pl.ds(4 + step, 16, stride=8), :]


def weigh(g, lat_weight):
    shape = jax.ShapeDtypeStruct((4, 64, 256), jnp.float32)
    return pl.pallas_call(
        weigh_kernel,
        out_shape=(shape, shape),
        in_specs=[pl.BlockSpec(memory_space=pltpu.VMEM)] * 2,
        out_specs=(pl.BlockSpec(memory_space=pltpu.VMEM),) * 2,
        scratch_shapes=[pltpu.VMEM((2, 128, 128), jnp.float32)],
        compiler_params=pltpu.CompilerParams(vmem_limit_bytes=16 << 20),
        cost_estimate=pl.CostEstimate(flops=1 << 18, bytes_accessed=1 << 20, transcendentals=0),
        name="weigh",
    )(g, lat_weight.reshape(1, 256))


def per_device(grid_field, lat_weight):
    y = lax.all_to_all(grid_field.reshape(16, 64, 128), "lon", 0, 0, tiled=True)
    z = transform(y)
    g = lax.all_to_all(z.reshape(256, 4, 128), ("lat", "lon"), 0, 0, tiled=True)
    real, imag = weigh(g.reshape(1024, 128), lat_weight)
    return tuple(part.transpose(0, 2, 1)[:, :, None, :] for part in (real, imag))


def solution(mesh):
    in_specs = (P(None, "lat", None, "lon"), P())
    out_specs = (P(None, None, "lat", "lon"), P(None, None, "lat", "lon"))
    return jax.shard_map(per_device, mesh=mesh, in_specs=in_specs, out_specs=out_specs, check_vma=False)
```

time: 160 us -> 61.8 us (0.39)
  waiting for transfers between devices: 105 us -> 0 us
  blocking collectives: 18.1 us -> 57.4 us
  between operations: 14.1 us -> 0.64 us
  matrix products: 13 us -> 0 us
  local copies, waits for them, and re-layouts: 7.7 us -> 1.59 us
  other arithmetic: 2.04 us -> 0 us
  Pallas kernels: 0 us -> 1.89 us
    reduce_scatter x1 -> x0, waiting for transfers between devices: 105 us -> none  [per_device(): lax.psum_scatter(lax.dot_general(dft_table, flat_grid, (((0,), (1,)), (()...]
    all_to_all x1 -> x2, blocking collectives: 18.1 us -> 57.4 us  [the longest x1 33.6 us: per_device(): g = lax.all_to_all(z.reshape(256, 4, 128), ('lat', 'lon'), 0, 0, tiled=True)]
    dot_general x1 -> x0, matrix products: 13 us -> none  [per_device(): lax.dot_general(dft_table, flat_grid, (((0,), (1,)), ((), ())), precision...]
    unnamed x8 -> x4, local copies, waits for them, and re-layouts: 4.59 us -> 1.59 us
    pallas_call x0 -> x2, Pallas kernels: none -> 1.89 us  [the longest x1 1.03 us: weigh(): pl.pallas_call(weigh_kernel, out_shape=(shape, shape), in_specs=[pl.Block...]
    all_to_all x1 -> x0, other arithmetic: 1.89 us -> none  [per_device(): lax.all_to_all(spectra, 'lat', split_axis=2, concat_axis=1, tiled=True)]
  transfers between devices with their start and end apart: 1 -> 0, of which waited for: 1 -> 0; matrix products, arithmetic and copies ran while one was open for 0% -> 0% of each run, Pallas kernels for 0% -> 0%
where the time goes in v1:
time: 61.8 us; the launch traced here: 61.5 us
  blocking collectives  57.4 us (93%)
  Pallas kernels  1.89 us (3%)
  local copies, waits for them, and re-layouts  1.59 us (3%)
  between operations  0.64 us (1%)
    all_to_all x1, blocking collectives, per_device(): g = lax.all_to_all(z.reshape(256, 4, 128), ('lat', 'lon'), 0, 0, tiled=True)  33.6 us
    all_to_all x1, blocking collectives, per_device(): y = lax.all_to_all(grid_field.reshape(16, 64, 128), 'lon', 0, 0, tiled=True)  23.8 us
    unnamed x4, local copies, waits for them, and re-layouts  1.59 us

profile of v1, /device:TPU:1, one launch (start us, length us, event | category | flops | bytes accessed | tf_op | source)
XLA Modules:
  0.0 61.5 jit_solution(13909986145258855233)
XLA Ops:
  0.6 23.8 %all_to_all.10.y_ref = f32[16,64,128]{2,1,0:T(8,128)S(1)} all-to-all(f32[16,64,128]{2,1,0:T(8,128)} %bitcast.17), channel_id=1, replica_groups=mesh['lon'=16,'lat'=16] {'lon'}, dimensions={0} | all-to-all | bytes 1048576 | tf_op jit(solution)/shard_map/all_to_all | solution.py:152
  24.5 0.0 copy-start
  24.5 1.6 %copy-done = bf16[2,8,256,256]{3,2,1,0:T(8,128)(2,1)S(1)} copy-done((bf16[2,8,256,256]{3,2,1,0:T(8,128)(2,1)S(1)}, bf16[2,8,256,256]{3,2,1,0:T(8,128)(2,1)}, u32[]{:S(2)}) %copy-start) | copy-done | bytes 2097176
  26.1 0.0 copy-start.1
  26.1 0.9 %transform.1 = f32[1024,128]{1,0:T(8,128)S(1)} custom-call(f32[16,64,128]{2,1,0:T(8,128)S(1)} %all_to_all.10.y_ref, bf16[2,8,256,256]{3,2,1,0:T(8,128)(2,1)S(1)} %copy-done), custom_call_target="tpu_custom_call" | custom-call | flops 201326592 | bytes 3145728 | tf_op jit(solution)/shard_map/transform/pallas_call | solution.py:109
  26.9 33.6 %all_to_all.11 = f32[256,4,128]{2,1,0:T(4,128)S(1)} all-to-all(f32[256,4,128]{2,1,0:T(4,128)S(1)} %bitcast.15), channel_id=1, replica_groups=mesh['lon'=16,'lat'=16] {'lat','lon'}, dimensions={0} | all-to-all | bytes 1048576 | tf_op jit(solution)/shard_map/all_to_all | solution.py:154
  60.5 0.0 copy-done.1
  60.5 1.0 %weigh.1 = (f32[4,64,256]{2,1,0:T(8,128)}, f32[4,64,256]{2,1,0:T(8,128)}) custom-call(f32[1024,128]{1,0:T(8,128)S(1)} %bitcast.14, f32[1,256]{1,0:T(1,128)S(1)} %bitcast.16), custom_call_target="tpu_custom_call" | custom-call | flops 262144 | bytes 1048576 | tf_op jit(solution)/shard_map/weigh/pallas_call | solution.py:139
Async XLA Ops:
  24.5 1.6 %copy-start = (bf16[2,8,256,256]{3,2,1,0:T(8,128)(2,1)S(1)}, bf16[2,8,256,256]{3,2,1,0:T(8,128)(2,1)}, u32[]{:S(2)}) copy-start(bf16[2,8,256,256]{3,2,1,0:T(8,128)(2,1)} %constant.2.clone.table_ref) | copy-start | bytes 6291460
  26.1 34.5 %copy-start.1 = (f32[256]{0:T(256)S(1)}, f32[256]{0:T(256)}, u32[]{:S(2)}) copy-start(f32[256]{0:T(256)} %param.4) | copy-start | bytes 3076

commit v2 on v1

--- a/solution.py
+++ b/solution.py
@@ -105,7 +105,26 @@
             o_ref[pl.ds(radius * 64 + j * 4 + latitude, 8, stride=64), :] = value
 
 
-def transform(y):
+def stage_kernel(table_ref, o_ref, sem):
+    copy = pltpu.make_async_copy(table_ref, o_ref, sem)
+    copy.start()
+    copy.wait()
+
+
+def stage(table):
+    return pl.pallas_call(
+        stage_kernel,
+        out_shape=jax.ShapeDtypeStruct(table.shape, table.dtype),
+        in_specs=[pl.BlockSpec(memory_space=pl.ANY)],
+        out_specs=pl.BlockSpec(memory_space=pltpu.VMEM),
+        scratch_shapes=[pltpu.SemaphoreType.DMA],
+        compiler_params=pltpu.CompilerParams(vmem_limit_bytes=4 << 20),
+        cost_estimate=pl.CostEstimate(flops=1 << 24, bytes_accessed=4 << 20, transcendentals=0),
+        name="stage",
+    )(table)
+
+
+def transform(y, table):
     return pl.pallas_call(
         transform_kernel,
         out_shape=jax.ShapeDtypeStruct((1024, 128), jnp.float32),
@@ -118,7 +137,7 @@
         compiler_params=pltpu.CompilerParams(vmem_limit_bytes=16 << 20),
         cost_estimate=pl.CostEstimate(flops=2 * 8 * 192 * 256 * 256, bytes_accessed=3 << 20, transcendentals=0),
         name="transform",
-    )(y, jnp.asarray(mode_tables()))
+    )(y, table)
 
 
 def weigh_kernel(g_ref, w_ref, re_ref, im_ref, turned):
@@ -150,7 +169,7 @@
 
 def per_device(grid_field, lat_weight):
     y = lax.all_to_all(grid_field.reshape(16, 64, 128), "lon", 0, 0, tiled=True)
-    z = transform(y)
+    z = transform(y, stage(jnp.asarray(mode_tables())))
     g = lax.all_to_all(z.reshape(256, 4, 128), ("lat", "lon"), 0, 0, tiled=True)
     real, imag = weigh(g.reshape(1024, 128), lat_weight)
     return tuple(part.transpose(0, 2, 1)[:, :, None, :] for part in (real, imag))

time: 61.8 us -> 60.2 us (0.974)
  blocking collectives: 57.4 us -> 33.6 us
  waiting for transfers between devices: 0 us -> 12 us
  starting transfers between devices: 0 us -> 10 us
    all_to_all x1 -> x0, blocking collectives: 23.8 us -> none  [per_device(): y = lax.all_to_all(grid_field.reshape(16, 64, 128), 'lon', 0, 0, tiled=True)]
    all_to_all x0 -> x1, waiting for transfers between devices: none -> 12 us  [per_device(): y = lax.all_to_all(grid_field.reshape(16, 64, 128), 'lon', 0, 0, tiled=True)]
    all_to_all x0 -> x1, starting transfers between devices: none -> 10 us  [per_device(): y = lax.all_to_all(grid_field.reshape(16, 64, 128), 'lon', 0, 0, tiled=True)]
  transfers between devices with their start and end apart: 0 -> 1, of which waited for: 0 -> 1; matrix products, arithmetic and copies ran while one was open for 0% -> 0% of each run, Pallas kernels for 0% -> 0%
where the time goes in v2:
time: 60.2 us; the launch traced here: 60 us
  blocking collectives  33.6 us (56%)
  waiting for transfers between devices  12 us (20%)
  starting transfers between devices  10 us (17%)
  Pallas kernels  2.06 us (3%)
  local copies, waits for them, and re-layouts  1.59 us (3%)
  between operations  0.67 us (1%)
    all_to_all x1, blocking collectives, per_device(): g = lax.all_to_all(z.reshape(256, 4, 128), ('lat', 'lon'), 0, 0, tiled=True)  33.6 us
    all_to_all x1, waiting for transfers between devices, per_device(): y = lax.all_to_all(grid_field.reshape(16, 64, 128), 'lon', 0, 0, tiled=True)  12 us
    all_to_all x1, starting transfers between devices, per_device(): y = lax.all_to_all(grid_field.reshape(16, 64, 128), 'lon', 0, 0, tiled=True)  10 us
    unnamed x4, local copies, waits for them, and re-layouts  1.59 us
  transfers between devices with their start and end apart: 1, of which 1 were waited for; matrix products, arithmetic and copies ran while one was open for 0% of the time, Pallas kernels for 0%

profile of v2, /device:TPU:1, one launch (start us, length us, event | category | flops | bytes accessed | tf_op | source)
XLA Modules:
  0.0 60.0 jit_solution(17167526578238516393)
XLA Ops:
  0.6 10.0 %all-to-all-start = ((f32[16,64,128]{2,1,0:T(8,128)}), f32[16,64,128]{2,1,0:T(8,128)S(1)}, u32[]{:S(2)}, u32[]{:S(2)}) async-start(f32[16,64,128]{2,1,0:T(8,128)} %bitcast.17), calls=%async_computation | async-start | bytes 1048576 | tf_op jit(solution)/shard_map/all_to_all | solution.py:171
  10.7 0.0 copy-start
  10.7 1.6 %copy-done = bf16[2,8,256,256]{3,2,1,0:T(8,128)(2,1)S(1)} copy-done((bf16[2,8,256,256]{3,2,1,0:T(8,128)(2,1)S(1)}, bf16[2,8,256,256]{3,2,1,0:T(8,128)(2,1)}, u32[]{:S(2)}) %copy-start) | copy-done | bytes 2097176
  12.3 0.1 stage.1.table_ref
  12.4 0.0 copy-start.1
  12.4 12.0 %all-to-all-done.y_ref = f32[16,64,128]{2,1,0:T(8,128)S(1)} async-done(((f32[16,64,128]{2,1,0:T(8,128)}), f32[16,64,128]{2,1,0:T(8,128)S(1)}, u32[]{:S(2)}, u32[]{:S(2)}) %all-to-all-start) | async-done | bytes 524320 | tf_op jit(solution)/shard_map/all_to_all | solution.py:171
  24.5 0.9 %transform.1 = f32[1024,128]{1,0:T(8,128)S(1)} custom-call(f32[16,64,128]{2,1,0:T(8,128)S(1)} %all-to-all-done.y_ref, bf16[2,8,256,256]{3,2,1,0:T(8,128)(2,1)S(1)} %stage.1.table_ref), custom_call_target="tpu_custom_call" | custom-call | flops 201326592 | bytes 3145728 | tf_op jit(solution)/shard_map/transform/pallas_call | solution.py:128
  25.4 33.6 %all_to_all.10 = f32[256,4,128]{2,1,0:T(4,128)S(1)} all-to-all(f32[256,4,128]{2,1,0:T(4,128)S(1)} %bitcast.15), channel_id=1, replica_groups=mesh['lon'=16,'lat'=16] {'lat','lon'}, dimensions={0} | all-to-all | bytes 1048576 | tf_op jit(solution)/shard_map/all_to_all | solution.py:173
  59.0 0.0 copy-done.1
  59.0 1.0 %weigh.1 = (f32[4,64,256]{2,1,0:T(8,128)}, f32[4,64,256]{2,1,0:T(8,128)}) custom-call(f32[1024,128]{1,0:T(8,128)S(1)} %bitcast.14, f32[1,256]{1,0:T(1,128)S(1)} %bitcast.16), custom_call_target="tpu_custom_call" | custom-call | flops 262144 | bytes 1048576 | tf_op jit(solution)/shard_map/weigh/pallas_call | solution.py:158
Async XLA Ops:
  0.6 23.8 %all-to-all-start = ((f32[16,64,128]{2,1,0:T(8,128)}), f32[16,64,128]{2,1,0:T(8,128)S(1)}, u32[]{:S(2)}, u32[]{:S(2)}) async-start(f32[16,64,128]{2,1,0:T(8,128)} %bitcast.17), calls=%async_computation | async-start | bytes 1048576 | tf_op jit(solution)/shard_map/all_to_all | solution.py:171
  10.7 1.6 %copy-start = (bf16[2,8,256,256]{3,2,1,0:T(8,128)(2,1)S(1)}, bf16[2,8,256,256]{3,2,1,0:T(8,128)(2,1)}, u32[]{:S(2)}) copy-start(bf16[2,8,256,256]{3,2,1,0:T(8,128)(2,1)} %constant.2.clone.table_ref) | copy-start | bytes 6291460
  12.4 46.5 %copy-start.1 = (f32[256]{0:T(256)S(1)}, f32[256]{0:T(256)}, u32[]{:S(2)}) copy-start(f32[256]{0:T(256)} %param.4) | copy-start | bytes 3076

commit v3 on v2

--- a/solution.py
+++ b/solution.py
@@ -12,6 +12,7 @@
 LENGTH = 2048
 PEERS = 16
 BLOCK = 128
+Z, FAR, NEAR, REST = 128, 64, 32, 4
 ROWS = 64
 
 
@@ -102,7 +103,8 @@
             value = v[-j % PEERS]
             if j:
                 value = pltpu.roll(value, 128 - 8 * j, 1)
-            o_ref[pl.ds(radius * 64 + j * 4 + latitude, 8, stride=64), :] = value
+            at = NEAR * (j // 8) + Z * (j % 8) + FAR * (radius // 8) + latitude
+            o_ref[pl.ds(at, 8, stride=REST), :] = value
 
 
 def stage_kernel(table_ref, o_ref, sem):
@@ -140,17 +142,28 @@
     )(y, table)
 
 
-def weigh_kernel(g_ref, w_ref, re_ref, im_ref, turned):
+def weigh_kernel(g_ref, w_ref, re_ref, im_ref, turned, real, imag, sems):
     weights = w_ref[...]
+    copies = []
     for f in range(4):
-        rows = jnp.concatenate([g_ref[64 * i + 16 * f : 64 * i + 16 * f + 16, :] for i in range(16)], axis=0)
         for half in range(2):
-            turned[half] = rows[128 * half : 128 * half + 128].T * weights[:, 128 * half : 128 * half + 128]
-        for half in range(2):
+            starts = [
+                NEAR * ((4 * f + q) // 8) + Z * ((4 * f + q) % 8) + FAR * half + REST * i
+                for i in range(8)
+                for q in range(4)
+            ]
+            rows = jnp.concatenate([g_ref[start : start + 4, :] for start in starts], axis=0)
             at = slice(128 * half, 128 * half + 128)
+            turned[f, half] = rows.T * weights[:, at]
             for step in range(4):
-                re_ref[f, 16 * step : 16 * step + 16, at] = turned[half, pl.ds(step, 16, stride=8), :]
-                im_ref[f, 16 * step : 16 * step + 16, at] = turned[half, pl.ds(4 + step, 16, stride=8), :]
+                real[f, 16 * step : 16 * step + 16, at] = turned[f, half, pl.ds(step, 16, stride=8), :]
+                imag[f, 16 * step : 16 * step + 16, at] = turned[f, half, pl.ds(4 + step, 16, stride=8), :]
+        copies.append(pltpu.make_async_copy(real.at[f], re_ref.at[f], sems.at[0, f]))
+        copies.append(pltpu.make_async_copy(imag.at[f], im_ref.at[f], sems.at[1, f]))
+        for copy in copies[-2:]:
+            copy.start()
+    for copy in copies:
+        copy.wait()
 
 
 def weigh(g, lat_weight):
@@ -159,8 +172,13 @@
         weigh_kernel,
         out_shape=(shape, shape),
         in_specs=[pl.BlockSpec(memory_space=pltpu.VMEM)] * 2,
-        out_specs=(pl.BlockSpec(memory_space=pltpu.VMEM),) * 2,
-        scratch_shapes=[pltpu.VMEM((2, 128, 128), jnp.float32)],
+        out_specs=(pl.BlockSpec(memory_space=pltpu.HBM),) * 2,
+        scratch_shapes=[
+            pltpu.VMEM((4, 2, 128, 128), jnp.float32),
+            pltpu.VMEM((4, 64, 256), jnp.float32),
+            pltpu.VMEM((4, 64, 256), jnp.float32),
+            pltpu.SemaphoreType.DMA((2, 4)),
+        ],
         compiler_params=pltpu.CompilerParams(vmem_limit_bytes=16 << 20),
         cost_estimate=pl.CostEstimate(flops=1 << 18, bytes_accessed=1 << 20, transcendentals=0),
         name="weigh",
@@ -168,14 +186,16 @@
 
 
 def per_device(grid_field, lat_weight):
-    y = lax.all_to_all(grid_field.reshape(16, 64, 128), "lon", 0, 0, tiled=True)
+    y = lax.all_to_all(grid_field.reshape(16, 64, 128), ("near", "z"), 0, 0, tiled=True)
     z = transform(y, stage(jnp.asarray(mode_tables())))
-    g = lax.all_to_all(z.reshape(256, 4, 128), ("lat", "lon"), 0, 0, tiled=True)
+    g = lax.all_to_all(z.reshape(256, 4, 128), ("z", "far", "near", "rest"), 0, 0, tiled=True)
     real, imag = weigh(g.reshape(1024, 128), lat_weight)
     return tuple(part.transpose(0, 2, 1)[:, :, None, :] for part in (real, imag))
 
 
 def solution(mesh):
-    in_specs = (P(None, "lat", None, "lon"), P())
-    out_specs = (P(None, None, "lat", "lon"), P(None, None, "lat", "lon"))
+    mesh = jax.sharding.Mesh(mesh.devices.reshape(2, 8, 2, 8), ("near", "z", "far", "rest"))
+    lon, lat = ("near", "z"), ("far", "rest")
+    in_specs = (P(None, lat, None, lon), P())
+    out_specs = (P(None, None, lat, lon), P(None, None, lat, lon))
     return jax.shard_map(per_device, mesh=mesh, in_specs=in_specs, out_specs=out_specs, check_vma=False)

time: 60.2 us -> 58.5 us (0.972)
  blocking collectives: 33.6 us -> 32.1 us
    all_to_all x1, blocking collectives: 33.6 us -> 32.1 us  [per_device(): lax.all_to_all(z.reshape(256, 4, 128), ('z', 'far', 'near', 'rest'), 0, 0...]
where the time goes in v3:
time: 58.5 us; the launch traced here: 58.3 us
  blocking collectives  32.1 us (55%)
  waiting for transfers between devices  12 us (21%)
  starting transfers between devices  10 us (17%)
  Pallas kernels  1.85 us (3%)
  local copies, waits for them, and re-layouts  1.59 us (3%)
  between operations  0.67 us (1%)
    all_to_all x1, blocking collectives, per_device(): lax.all_to_all(z.reshape(256, 4, 128), ('z', 'far', 'near', 'rest'), 0, 0...  32.1 us
    all_to_all x1, waiting for transfers between devices, per_device(): lax.all_to_all(grid_field.reshape(16, 64, 128), ('near', 'z'), 0, 0, tile...  12 us
    all_to_all x1, starting transfers between devices, per_device(): lax.all_to_all(grid_field.reshape(16, 64, 128), ('near', 'z'), 0, 0, tile...  10 us
    unnamed x4, local copies, waits for them, and re-layouts  1.59 us
  transfers between devices with their start and end apart: 1, of which 1 were waited for; matrix products, arithmetic and copies ran while one was open for 0% of the time, Pallas kernels for 0%

profile of v3, /device:TPU:1, one launch (start us, length us, event | category | flops | bytes accessed | tf_op | source)
XLA Modules:
  0.0 58.3 jit_solution(18201365267955103382)
XLA Ops:
  0.6 10.0 %all-to-all-start = ((f32[16,64,128]{2,1,0:T(8,128)}), f32[16,64,128]{2,1,0:T(8,128)S(1)}, u32[]{:S(2)}, u32[]{:S(2)}) async-start(f32[16,64,128]{2,1,0:T(8,128)} %bitcast.17), calls=%async_computation | async-start | bytes 1048576 | tf_op jit(solution)/shard_map/all_to_all | solution.py:189
  10.7 0.0 copy-start
  10.7 1.6 %copy-done = bf16[2,8,256,256]{3,2,1,0:T(8,128)(2,1)S(1)} copy-done((bf16[2,8,256,256]{3,2,1,0:T(8,128)(2,1)S(1)}, bf16[2,8,256,256]{3,2,1,0:T(8,128)(2,1)}, u32[]{:S(2)}) %copy-start) | copy-done | bytes 2097176
  12.3 0.1 stage.1.table_ref
  12.4 0.0 copy-start.1
  12.4 12.0 %all-to-all-done.y_ref = f32[16,64,128]{2,1,0:T(8,128)S(1)} async-done(((f32[16,64,128]{2,1,0:T(8,128)}), f32[16,64,128]{2,1,0:T(8,128)S(1)}, u32[]{:S(2)}, u32[]{:S(2)}) %all-to-all-start) | async-done | bytes 524320 | tf_op jit(solution)/shard_map/all_to_all | solution.py:189
  24.5 0.7 %transform.1 = f32[1024,128]{1,0:T(8,128)S(1)} custom-call(f32[16,64,128]{2,1,0:T(8,128)S(1)} %all-to-all-done.y_ref, bf16[2,8,256,256]{3,2,1,0:T(8,128)(2,1)S(1)} %stage.1.table_ref), custom_call_target="tpu_custom_call" | custom-call | flops 201326592 | bytes 3145728 | tf_op jit(solution)/shard_map/transform/pallas_call | solution.py:130
  25.2 32.1 %all_to_all.10 = f32[256,4,128]{2,1,0:T(4,128)S(1)} all-to-all(f32[256,4,128]{2,1,0:T(4,128)S(1)} %bitcast.15), channel_id=1, replica_groups=mesh['near'=2,'z'=8,'far'=2,'rest'=8] {'z','far','near','rest'}, dimensions={0} | all-to-all | bytes 1048576 | tf_op jit(solution)/shard_map/all_to_all | solution.py:191
  57.3 0.0 copy-done.1
  57.3 1.0 %weigh.1 = (f32[4,64,256]{2,1,0:T(8,128)}, f32[4,64,256]{2,1,0:T(8,128)}) custom-call(f32[1024,128]{1,0:T(8,128)S(1)} %bitcast.14, f32[1,256]{1,0:T(1,128)S(1)} %bitcast.16), custom_call_target="tpu_custom_call" | custom-call | flops 262144 | bytes 1048576 | tf_op jit(solution)/shard_map/weigh/pallas_call | solution.py:171
Async XLA Ops:
  0.6 23.8 %all-to-all-start = ((f32[16,64,128]{2,1,0:T(8,128)}), f32[16,64,128]{2,1,0:T(8,128)S(1)}, u32[]{:S(2)}, u32[]{:S(2)}) async-start(f32[16,64,128]{2,1,0:T(8,128)} %bitcast.17), calls=%async_computation | async-start | bytes 1048576 | tf_op jit(solution)/shard_map/all_to_all | solution.py:189
  10.7 1.6 %copy-start = (bf16[2,8,256,256]{3,2,1,0:T(8,128)(2,1)S(1)}, bf16[2,8,256,256]{3,2,1,0:T(8,128)(2,1)}, u32[]{:S(2)}) copy-start(bf16[2,8,256,256]{3,2,1,0:T(8,128)(2,1)} %constant.2.clone.table_ref) | copy-start | bytes 6291460
  12.4 44.9 %copy-start.1 = (f32[256]{0:T(256)S(1)}, f32[256]{0:T(256)}, u32[]{:S(2)}) copy-start(f32[256]{0:T(256)} %param.4) | copy-start | bytes 3076

commit v4 on v3

--- a/solution.py
+++ b/solution.py
@@ -14,6 +14,9 @@
 BLOCK = 128
 Z, FAR, NEAR, REST = 128, 64, 32, 4
 ROWS = 64
+
+
+ORDER = [8 * near + (z + 4) % 8 for near in range(2) for z in range(8)]
 
 
 def mode_tables():
@@ -77,7 +80,7 @@
 def transform_kernel(y_ref, table_ref, o_ref, lhs, mid):
     for g in range(ROWS // 16):
         rows = slice(16 * g, 16 * g + 16)
-        dft = real_dft16([y_ref[a, rows, :] for a in range(PEERS)])
+        dft = real_dft16([y_ref[ORDER.index(a), rows, :] for a in range(PEERS)])
         for tile in range(8):
             pair = (dft[0][0], dft[8][0]) if tile == 0 else dft[tile]
             for part in range(2):
@@ -148,7 +151,7 @@
     for f in range(4):
         for half in range(2):
             starts = [
-                NEAR * ((4 * f + q) // 8) + Z * ((4 * f + q) % 8) + FAR * half + REST * i
+                NEAR * (ORDER[4 * f + q] // 8) + Z * (ORDER[4 * f + q] % 8) + FAR * half + REST * i
                 for i in range(8)
                 for q in range(4)
             ]
@@ -186,9 +189,9 @@
 
 
 def per_device(grid_field, lat_weight):
-    y = lax.all_to_all(grid_field.reshape(16, 64, 128), ("near", "z"), 0, 0, tiled=True)
+    y = lax.all_to_all(grid_field.reshape(16, 64, 128), ("near", "z"), 0, 0, tiled=True, axis_index_groups=[ORDER])
     z = transform(y, stage(jnp.asarray(mode_tables())))
-    g = lax.all_to_all(z.reshape(256, 4, 128), ("z", "far", "near", "rest"), 0, 0, tiled=True)
+    g = lax.all_to_all(z.reshape(256, 1, 512), ("z", "far", "near", "rest"), 0, 0, tiled=True)
     real, imag = weigh(g.reshape(1024, 128), lat_weight)
     return tuple(part.transpose(0, 2, 1)[:, :, None, :] for part in (real, imag))
 

time: 58.5 us -> 57.8 us (0.988)
  starting transfers between devices: 10 us -> 11.6 us
  waiting for transfers between devices: 12 us -> 10.6 us
  blocking collectives: 32.1 us -> 31.3 us
    all_to_all x1, starting transfers between devices: 10 us -> 11.6 us  [per_device(): lax.all_to_all(grid_field.reshape(16, 64, 128), ('near', 'z'), 0, 0, tile...]
    all_to_all x1, waiting for transfers between devices: 12 us -> 10.6 us  [per_device(): lax.all_to_all(grid_field.reshape(16, 64, 128), ('near', 'z'), 0, 0, tile...]
    all_to_all x1, blocking collectives: 32.1 us -> 31.3 us  [per_device(): lax.all_to_all(z.reshape(256, 1, 512), ('z', 'far', 'near', 'rest'), 0, 0...]
where the time goes in v4:
time: 57.8 us; the launch traced here: 57.5 us
  blocking collectives  31.3 us (54%)
  starting transfers between devices  11.6 us (20%)
  waiting for transfers between devices  10.6 us (18%)
  Pallas kernels  1.86 us (3%)
  local copies, waits for them, and re-layouts  1.59 us (3%)
  between operations  0.66 us (1%)
    all_to_all x1, blocking collectives, per_device(): lax.all_to_all(z.reshape(256, 1, 512), ('z', 'far', 'near', 'rest'), 0, 0...  31.3 us
    all_to_all x1, starting transfers between devices, per_device(): lax.all_to_all(grid_field.reshape(16, 64, 128), ('near', 'z'), 0, 0, tile...  11.6 us
    all_to_all x1, waiting for transfers between devices, per_device(): lax.all_to_all(grid_field.reshape(16, 64, 128), ('near', 'z'), 0, 0, tile...  10.6 us
    unnamed x4, local copies, waits for them, and re-layouts  1.59 us
  transfers between devices with their start and end apart: 1, of which 1 were waited for; matrix products, arithmetic and copies ran while one was open for 0% of the time, Pallas kernels for 0%

profile of v4, /device:TPU:1, one launch (start us, length us, event | category | flops | bytes accessed | tf_op | source)
XLA Modules:
  0.0 57.5 jit_solution(13230231370732911164)
XLA Ops:
  0.6 11.6 %all-to-all-start = ((f32[16,64,128]{2,1,0:T(8,128)}), f32[16,64,128]{2,1,0:T(8,128)S(1)}, u32[]{:S(2)}, u32[]{:S(2)}) async-start(f32[16,64,128]{2,1,0:T(8,128)} %bitcast.17), calls=%async_computation | async-start | bytes 1048576 | tf_op jit(solution)/shard_map/all_to_all | solution.py:192
  12.2 0.0 copy-start
  12.2 1.6 %copy-done = bf16[2,8,256,256]{3,2,1,0:T(8,128)(2,1)S(1)} copy-done((bf16[2,8,256,256]{3,2,1,0:T(8,128)(2,1)S(1)}, bf16[2,8,256,256]{3,2,1,0:T(8,128)(2,1)}, u32[]{:S(2)}) %copy-start) | copy-done | bytes 2097176
  13.8 0.1 stage.1.table_ref
  14.0 0.0 copy-start.1
  14.0 10.6 %all-to-all-done.y_ref = f32[16,64,128]{2,1,0:T(8,128)S(1)} async-done(((f32[16,64,128]{2,1,0:T(8,128)}), f32[16,64,128]{2,1,0:T(8,128)S(1)}, u32[]{:S(2)}, u32[]{:S(2)}) %all-to-all-start) | async-done | bytes 524320 | tf_op jit(solution)/shard_map/all_to_all | solution.py:192
  24.6 0.7 %transform.1 = f32[1024,128]{1,0:T(8,128)S(1)} custom-call(f32[16,64,128]{2,1,0:T(8,128)S(1)} %all-to-all-done.y_ref, bf16[2,8,256,256]{3,2,1,0:T(8,128)(2,1)S(1)} %stage.1.table_ref), custom_call_target="tpu_custom_call" | custom-call | flops 201326592 | bytes 3145728 | tf_op jit(solution)/shard_map/transform/pallas_call | solution.py:133
  25.3 31.3 %all_to_all.10 = f32[256,1,512]{2,1,0:T(1,128)S(1)} all-to-all(f32[256,1,512]{2,1,0:T(1,128)S(1)} %bitcast.15), channel_id=1, replica_groups=mesh['near'=2,'z'=8,'far'=2,'rest'=8] {'z','far','near','rest'}, dimensions={0} | all-to-all | bytes 1048576 | tf_op jit(solution)/shard_map/all_to_all | solution.py:194
  56.6 0.0 copy-done.1
  56.6 1.0 %weigh.1 = (f32[4,64,256]{2,1,0:T(8,128)}, f32[4,64,256]{2,1,0:T(8,128)}) custom-call(f32[1024,128]{1,0:T(8,128)S(1)} %bitcast.14, f32[1,256]{1,0:T(1,128)S(1)} %bitcast.16), custom_call_target="tpu_custom_call" | custom-call | flops 262144 | bytes 1048576 | tf_op jit(solution)/shard_map/weigh/pallas_call | solution.py:174
Async XLA Ops:
  0.6 23.9 %all-to-all-start = ((f32[16,64,128]{2,1,0:T(8,128)}), f32[16,64,128]{2,1,0:T(8,128)S(1)}, u32[]{:S(2)}, u32[]{:S(2)}) async-start(f32[16,64,128]{2,1,0:T(8,128)} %bitcast.17), calls=%async_computation | async-start | bytes 1048576 | tf_op jit(solution)/shard_map/all_to_all | solution.py:192
  12.2 1.6 %copy-start = (bf16[2,8,256,256]{3,2,1,0:T(8,128)(2,1)S(1)}, bf16[2,8,256,256]{3,2,1,0:T(8,128)(2,1)}, u32[]{:S(2)}) copy-start(bf16[2,8,256,256]{3,2,1,0:T(8,128)(2,1)} %constant.2.clone.table_ref) | copy-start | bytes 6291460
  14.0 42.6 %copy-start.1 = (f32[256]{0:T(256)S(1)}, f32[256]{0:T(256)}, u32[]{:S(2)}) copy-start(f32[256]{0:T(256)} %param.4) | copy-start | bytes 3076

commit v5 on v3

--- a/solution.py
+++ b/solution.py
@@ -12,8 +12,27 @@
 LENGTH = 2048
 PEERS = 16
 BLOCK = 128
-Z, FAR, NEAR, REST = 128, 64, 32, 4
 ROWS = 64
+
+
+LON = [8 * near + (z + 4) % 8 for near in range(2) for z in range(8)]
+FARS = [1, 0]
+
+
+def place(rest, lon):
+    near, z = divmod(lon, 8)
+    return 8 * ((z - 4) % 8) + 64 * near + 1 * ((rest - 4) % 8)
+
+
+def first():
+    return [[16 * far + lon for far in FARS for lon in LON]]
+
+
+def second():
+    order = np.empty(128, np.int64)
+    for device, parts in enumerate(np.ndindex(8, 16)):
+        order[place(*parts)] = device
+    return [[int(device) for device in order]]
 
 
 def mode_tables():
@@ -76,8 +95,8 @@
 
 def transform_kernel(y_ref, table_ref, o_ref, lhs, mid):
     for g in range(ROWS // 16):
-        rows = slice(16 * g, 16 * g + 16)
-        dft = real_dft16([y_ref[a, rows, :] for a in range(PEERS)])
+        far, inner = divmod(16 * g, 32)
+        dft = real_dft16([y_ref[FARS.index(far) * PEERS + LON.index(a), inner : inner + 16, :] for a in range(PEERS)])
         for tile in range(8):
             pair = (dft[0][0], dft[8][0]) if tile == 0 else dft[tile]
             for part in range(2):
@@ -98,13 +117,12 @@
         v = [mid[k, 8 * g : 8 * g + 8, :] for k in range(PEERS)]
         for s in range(4):
             v = [jnp.where(bits[s], v[(i + (1 << s)) % PEERS], v[i]) for i in range(PEERS)]
-        latitude, radius = g // 2, 8 * (g % 2)
         for j in range(PEERS):
             value = v[-j % PEERS]
             if j:
                 value = pltpu.roll(value, 128 - 8 * j, 1)
-            at = NEAR * (j // 8) + Z * (j % 8) + FAR * (radius // 8) + latitude
-            o_ref[pl.ds(at, 8, stride=REST), :] = value
+            for rest in (0, 4):
+                o_ref[pl.ds(8 * place(rest, j) + g, 4, stride=8), :] = value[rest : rest + 4]
 
 
 def stage_kernel(table_ref, o_ref, sem):
@@ -147,11 +165,7 @@
     copies = []
     for f in range(4):
         for half in range(2):
-            starts = [
-                NEAR * ((4 * f + q) // 8) + Z * ((4 * f + q) % 8) + FAR * half + REST * i
-                for i in range(8)
-                for q in range(4)
-            ]
+            starts = [8 * place(i, LON[4 * f + q]) + 4 * half for i in range(8) for q in range(4)]
             rows = jnp.concatenate([g_ref[start : start + 4, :] for start in starts], axis=0)
             at = slice(128 * half, 128 * half + 128)
             turned[f, half] = rows.T * weights[:, at]
@@ -186,16 +200,17 @@
 
 
 def per_device(grid_field, lat_weight):
-    y = lax.all_to_all(grid_field.reshape(16, 64, 128), ("near", "z"), 0, 0, tiled=True)
-    z = transform(y, stage(jnp.asarray(mode_tables())))
-    g = lax.all_to_all(z.reshape(256, 4, 128), ("z", "far", "near", "rest"), 0, 0, tiled=True)
+    table = stage(jnp.asarray(mode_tables()))
+    y = lax.all_to_all(grid_field.reshape(64, 2, 8, 128)[:, ::-1].transpose(1, 0, 2, 3).reshape(32, 32, 128), ("far", "lon"), 0, 0, tiled=True, axis_index_groups=first())
+    z = transform(y, table)
+    g = lax.all_to_all(z.reshape(128, 8, 128), ("near", "lon"), 0, 0, tiled=True, axis_index_groups=second())
     real, imag = weigh(g.reshape(1024, 128), lat_weight)
     return tuple(part.transpose(0, 2, 1)[:, :, None, :] for part in (real, imag))
 
 
 def solution(mesh):
-    mesh = jax.sharding.Mesh(mesh.devices.reshape(2, 8, 2, 8), ("near", "z", "far", "rest"))
-    lon, lat = ("near", "z"), ("far", "rest")
-    in_specs = (P(None, lat, None, lon), P())
-    out_specs = (P(None, None, lat, lon), P(None, None, lat, lon))
+    mesh = jax.sharding.Mesh(mesh.devices.reshape(16, 2, 8), ("lon", "far", "near"))
+    lat = ("far", "near")
+    in_specs = (P(None, lat, None, "lon"), P())
+    out_specs = (P(None, None, lat, "lon"), P(None, None, lat, "lon"))
     return jax.shard_map(per_device, mesh=mesh, in_specs=in_specs, out_specs=out_specs, check_vma=False)

time: 58.5 us -> 56.5 us (0.966)
  blocking collectives: 32.1 us -> 26.5 us
  starting transfers between devices: 10 us -> 13.9 us
  waiting for transfers between devices: 12 us -> 9.78 us
  local copies, waits for them, and re-layouts: 1.59 us -> 3.5 us
    all_to_all x1, blocking collectives: 32.1 us -> 26.5 us  [per_device(): lax.all_to_all(z.reshape(128, 8, 128), ('near', 'lon'), 0, 0, tiled=True,...]
    all_to_all x1, starting transfers between devices: 10 us -> 13.9 us  [per_device(): lax.all_to_all(grid_field.reshape(64, 2, 8, 128)[:, ::-1].transpose(1, 0,...]
    all_to_all x1, waiting for transfers between devices: 12 us -> 9.78 us  [per_device(): lax.all_to_all(grid_field.reshape(64, 2, 8, 128)[:, ::-1].transpose(1, 0,...]
    reshape x0 -> x1, local copies, waits for them, and re-layouts: none -> 1.08 us  [per_device(): grid_field.reshape(64, 2, 8, 128)[:, ::-1].transpose(1, 0, 2, 3)]
    rev x0 -> x1, local copies, waits for them, and re-layouts: none -> 0.83 us  [per_device(): grid_field.reshape(64, 2, 8, 128)[:, ::-1].transpose(1, 0, 2, 3)]
where the time goes in v5:
time: 56.5 us; the launch traced here: 56.2 us
  blocking collectives  26.5 us (47%)
  starting transfers between devices  13.9 us (25%)
  waiting for transfers between devices  9.78 us (17%)
  local copies, waits for them, and re-layouts  3.5 us (6%)
  Pallas kernels  1.84 us (3%)
  between operations  0.67 us (1%)
    all_to_all x1, blocking collectives, per_device(): lax.all_to_all(z.reshape(128, 8, 128), ('near', 'lon'), 0, 0, tiled=True,...  26.5 us
    all_to_all x1, starting transfers between devices, per_device(): lax.all_to_all(grid_field.reshape(64, 2, 8, 128)[:, ::-1].transpose(1, 0,...  13.9 us
    all_to_all x1, waiting for transfers between devices, per_device(): lax.all_to_all(grid_field.reshape(64, 2, 8, 128)[:, ::-1].transpose(1, 0,...  9.78 us
    unnamed x4, local copies, waits for them, and re-layouts  1.59 us
  transfers between devices with their start and end apart: 1, of which 1 were waited for; matrix products, arithmetic and copies ran while one was open for 0% of the time, Pallas kernels for 0%

profile of v5, /device:TPU:1, one launch (start us, length us, event | category | flops | bytes accessed | tf_op | source)
XLA Modules:
  0.0 56.2 jit_solution(11553609272661677979)
XLA Ops:
  0.6 1.1 %copy.5 = f32[64,2,8,128]{3,2,0,1:T(8,128)S(1)} copy(f32[64,2,8,128]{3,2,1,0:T(8,128)} %bitcast.20) | data formatting | bytes 1048576 | tf_op jit(solution)/shard_map/reshape | solution.py:204
  1.7 0.8 %rev.3 = f32[64,2,8,128]{3,2,0,1:T(8,128)} reverse(f32[64,2,8,128]{3,2,0,1:T(8,128)S(1)} %copy.5), dimensions={1} | reverse | bytes 1048576 | tf_op jit(solution)/shard_map/rev | solution.py:204
  2.5 13.9 %all-to-all-start = ((f32[32,32,128]{2,1,0:T(8,128)}), f32[32,32,128]{2,1,0:T(8,128)S(1)}, u32[]{:S(2)}, u32[]{:S(2)}) async-start(f32[32,32,128]{2,1,0:T(8,128)} %bitcast.2), calls=%async_computation | async-start | bytes 1048576 | tf_op jit(solution)/shard_map/all_to_all | solution.py:204
  16.5 0.0 copy-start
  16.5 1.6 %copy-done = bf16[2,8,256,256]{3,2,1,0:T(8,128)(2,1)S(1)} copy-done((bf16[2,8,256,256]{3,2,1,0:T(8,128)(2,1)S(1)}, bf16[2,8,256,256]{3,2,1,0:T(8,128)(2,1)}, u32[]{:S(2)}) %copy-start) | copy-done | bytes 2097176
  18.1 0.1 stage.1.table_ref
  18.2 0.0 copy-start.1
  18.2 9.8 %all-to-all-done.y_ref = f32[32,32,128]{2,1,0:T(8,128)S(1)} async-done(((f32[32,32,128]{2,1,0:T(8,128)}), f32[32,32,128]{2,1,0:T(8,128)S(1)}, u32[]{:S(2)}, u32[]{:S(2)}) %all-to-all-start) | async-done | bytes 524320 | tf_op jit(solution)/shard_map/all_to_all | solution.py:204
  28.0 0.7 %transform.1 = f32[1024,128]{1,0:T(8,128)S(1)} custom-call(f32[32,32,128]{2,1,0:T(8,128)S(1)} %all-to-all-done.y_ref, bf16[2,8,256,256]{3,2,1,0:T(8,128)(2,1)S(1)} %stage.1.table_ref), custom_call_target="tpu_custom_call" | custom-call | flops 201326592 | bytes 3145728 | tf_op jit(solution)/shard_map/transform/pallas_call | solution.py:148
  28.7 26.5 %all_to_all.10 = f32[128,8,128]{2,1,0:T(8,128)S(1)} all-to-all(f32[128,8,128]{2,1,0:T(8,128)S(1)} %bitcast.18), channel_id=1, replica_groups={{68,69,70,71,64,65,66,67,84,85,86,87,80,81,82,83,100,101,102,103,96,97,..., dimensions={0} | all-to-all | bytes 1048576 | tf_op jit(solution)/shard_map/all_to_all | solution.py:206
  55.2 0.0 copy-done.1
  55.2 1.0 %weigh.1 = (f32[4,64,256]{2,1,0:T(8,128)}, f32[4,64,256]{2,1,0:T(8,128)}) custom-call(f32[1024,128]{1,0:T(8,128)S(1)} %bitcast.17, f32[1,256]{1,0:T(1,128)S(1)} %bitcast.19), custom_call_target="tpu_custom_call" | custom-call | flops 262144 | bytes 1048576 | tf_op jit(solution)/shard_map/weigh/pallas_call | solution.py:185
Async XLA Ops:
  2.5 25.5 %all-to-all-start = ((f32[32,32,128]{2,1,0:T(8,128)}), f32[32,32,128]{2,1,0:T(8,128)S(1)}, u32[]{:S(2)}, u32[]{:S(2)}) async-start(f32[32,32,128]{2,1,0:T(8,128)} %bitcast.2), calls=%async_computation | async-start | bytes 1048576 | tf_op jit(solution)/shard_map/all_to_all | solution.py:204
  16.5 1.6 %copy-start = (bf16[2,8,256,256]{3,2,1,0:T(8,128)(2,1)S(1)}, bf16[2,8,256,256]{3,2,1,0:T(8,128)(2,1)}, u32[]{:S(2)}) copy-start(bf16[2,8,256,256]{3,2,1,0:T(8,128)(2,1)} %constant.2.clone.table_ref) | copy-start | bytes 6291460
  18.2 37.0 %copy-start.1 = (f32[256]{0:T(256)S(1)}, f32[256]{0:T(256)}, u32[]{:S(2)}) copy-start(f32[256]{0:T(256)} %param.4) | copy-start | bytes 3076

commit v6 on v5

--- a/solution.py
+++ b/solution.py
@@ -14,14 +14,13 @@
 BLOCK = 128
 ROWS = 64
 
-
 LON = [8 * near + (z + 4) % 8 for near in range(2) for z in range(8)]
 FARS = [1, 0]
 
 
 def place(rest, lon):
     near, z = divmod(lon, 8)
-    return 8 * ((z - 4) % 8) + 64 * near + 1 * ((rest - 4) % 8)
+    return 16 * ((z - 4) % 8) + 8 * (1 - near) + (rest - 5) % 8
 
 
 def first():
@@ -121,8 +120,8 @@
             value = v[-j % PEERS]
             if j:
                 value = pltpu.roll(value, 128 - 8 * j, 1)
-            for rest in (0, 4):
-                o_ref[pl.ds(8 * place(rest, j) + g, 4, stride=8), :] = value[rest : rest + 4]
+            for rest, end in ((0, 5), (5, 8)):
+                o_ref[pl.ds(8 * place(rest, j) + g, end - rest, stride=8), :] = value[rest:end]
 
 
 def stage_kernel(table_ref, o_ref, sem):
@@ -201,7 +200,8 @@
 
 def per_device(grid_field, lat_weight):
     table = stage(jnp.asarray(mode_tables()))
-    y = lax.all_to_all(grid_field.reshape(64, 2, 8, 128)[:, ::-1].transpose(1, 0, 2, 3).reshape(32, 32, 128), ("far", "lon"), 0, 0, tiled=True, axis_index_groups=first())
+    x = grid_field.reshape(64, 2, 8, 128)[:, ::-1].transpose(1, 0, 2, 3).reshape(32, 32, 128)
+    y = lax.all_to_all(x, ("far", "lon"), 0, 0, tiled=True, axis_index_groups=first())
     z = transform(y, table)
     g = lax.all_to_all(z.reshape(128, 8, 128), ("near", "lon"), 0, 0, tiled=True, axis_index_groups=second())
     real, imag = weigh(g.reshape(1024, 128), lat_weight)

time: 56.5 us -> 55.9 us (0.989)
  blocking collectives: 26.5 us -> 25.9 us
where the time goes in v6:
time: 55.9 us; the launch traced here: 55.7 us
  blocking collectives  25.9 us (46%)
  starting transfers between devices  13.9 us (25%)
  waiting for transfers between devices  9.78 us (17%)
  local copies, waits for them, and re-layouts  3.5 us (6%)
  Pallas kernels  1.84 us (3%)
  between operations  0.67 us (1%)
    all_to_all x1, blocking collectives, per_device(): lax.all_to_all(z.reshape(128, 8, 128), ('near', 'lon'), 0, 0, tiled=True,...  25.9 us
    all_to_all x1, starting transfers between devices, per_device(): lax.all_to_all(x, ('far', 'lon'), 0, 0, tiled=True, axis_index_groups=fir...  13.9 us
    all_to_all x1, waiting for transfers between devices, per_device(): lax.all_to_all(x, ('far', 'lon'), 0, 0, tiled=True, axis_index_groups=fir...  9.78 us
    unnamed x4, local copies, waits for them, and re-layouts  1.59 us
  transfers between devices with their start and end apart: 1, of which 1 were waited for; matrix products, arithmetic and copies ran while one was open for 0% of the time, Pallas kernels for 0%

profile of v6, /device:TPU:1, one launch (start us, length us, event | category | flops | bytes accessed | tf_op | source)
XLA Modules:
  0.0 55.7 jit_solution(10678283587167528546)
XLA Ops:
  0.6 1.1 %copy.5 = f32[64,2,8,128]{3,2,0,1:T(8,128)S(1)} copy(f32[64,2,8,128]{3,2,1,0:T(8,128)} %bitcast.20) | data formatting | bytes 1048576 | tf_op jit(solution)/shard_map/reshape | solution.py:203
  1.7 0.8 %rev.3 = f32[64,2,8,128]{3,2,0,1:T(8,128)} reverse(f32[64,2,8,128]{3,2,0,1:T(8,128)S(1)} %copy.5), dimensions={1} | reverse | bytes 1048576 | tf_op jit(solution)/shard_map/rev | solution.py:203
  2.5 13.9 %all-to-all-start = ((f32[32,32,128]{2,1,0:T(8,128)}), f32[32,32,128]{2,1,0:T(8,128)S(1)}, u32[]{:S(2)}, u32[]{:S(2)}) async-start(f32[32,32,128]{2,1,0:T(8,128)} %bitcast.2), calls=%async_computation | async-start | bytes 1048576 | tf_op jit(solution)/shard_map/all_to_all | solution.py:204
  16.5 0.0 copy-start
  16.5 1.6 %copy-done = bf16[2,8,256,256]{3,2,1,0:T(8,128)(2,1)S(1)} copy-done((bf16[2,8,256,256]{3,2,1,0:T(8,128)(2,1)S(1)}, bf16[2,8,256,256]{3,2,1,0:T(8,128)(2,1)}, u32[]{:S(2)}) %copy-start) | copy-done | bytes 2097176
  18.1 0.1 stage.1.table_ref
  18.2 0.0 copy-start.1
  18.2 9.8 %all-to-all-done.y_ref = f32[32,32,128]{2,1,0:T(8,128)S(1)} async-done(((f32[32,32,128]{2,1,0:T(8,128)}), f32[32,32,128]{2,1,0:T(8,128)S(1)}, u32[]{:S(2)}, u32[]{:S(2)}) %all-to-all-start) | async-done | bytes 524320 | tf_op jit(solution)/shard_map/all_to_all | solution.py:204
  28.0 0.7 %transform.1 = f32[1024,128]{1,0:T(8,128)S(1)} custom-call(f32[32,32,128]{2,1,0:T(8,128)S(1)} %all-to-all-done.y_ref, bf16[2,8,256,256]{3,2,1,0:T(8,128)(2,1)S(1)} %stage.1.table_ref), custom_call_target="tpu_custom_call" | custom-call | flops 201326592 | bytes 3145728 | tf_op jit(solution)/shard_map/transform/pallas_call | solution.py:147
  28.7 25.9 %all_to_all.10 = f32[128,8,128]{2,1,0:T(8,128)S(1)} all-to-all(f32[128,8,128]{2,1,0:T(8,128)S(1)} %bitcast.18), channel_id=1, replica_groups={{197,198,199,192,193,194,195,196,69,70,71,64,65,66,67,68,213,214,215,20..., dimensions={0} | all-to-all | bytes 1048576 | tf_op jit(solution)/shard_map/all_to_all | solution.py:206
  54.7 0.0 copy-done.1
  54.7 1.0 %weigh.1 = (f32[4,64,256]{2,1,0:T(8,128)}, f32[4,64,256]{2,1,0:T(8,128)}) custom-call(f32[1024,128]{1,0:T(8,128)S(1)} %bitcast.17, f32[1,256]{1,0:T(1,128)S(1)} %bitcast.19), custom_call_target="tpu_custom_call" | custom-call | flops 262144 | bytes 1048576 | tf_op jit(solution)/shard_map/weigh/pallas_call | solution.py:184
Async XLA Ops:
  2.5 25.5 %all-to-all-start = ((f32[32,32,128]{2,1,0:T(8,128)}), f32[32,32,128]{2,1,0:T(8,128)S(1)}, u32[]{:S(2)}, u32[]{:S(2)}) async-start(f32[32,32,128]{2,1,0:T(8,128)} %bitcast.2), calls=%async_computation | async-start | bytes 1048576 | tf_op jit(solution)/shard_map/all_to_all | solution.py:204
  16.5 1.6 %copy-start = (bf16[2,8,256,256]{3,2,1,0:T(8,128)(2,1)S(1)}, bf16[2,8,256,256]{3,2,1,0:T(8,128)(2,1)}, u32[]{:S(2)}) copy-start(bf16[2,8,256,256]{3,2,1,0:T(8,128)(2,1)} %constant.2.clone.table_ref) | copy-start | bytes 6291460
  18.2 36.5 %copy-start.1 = (f32[256]{0:T(256)S(1)}, f32[256]{0:T(256)}, u32[]{:S(2)}) copy-start(f32[256]{0:T(256)} %param.4) | copy-start | bytes 3076

commit v7 on v6

--- a/solution.py
+++ b/solution.py
@@ -159,6 +159,37 @@
     )(y, table)
 
 
+def pack_kernel(x_ref, o_ref, held, sems):
+    pieces = [(i, slice(16 * part, 16 * part + 16)) for part in range(4) for i in range(2)]
+    ins = [
+        pltpu.make_async_copy(x_ref.at[rows, FARS[i]], held.at[i, rows], sems.at[0, n])
+        for n, (i, rows) in enumerate(pieces)
+    ]
+    outs = [
+        pltpu.make_async_copy(held.at[i, rows], o_ref.at[i, rows], sems.at[1, n]) for n, (i, rows) in enumerate(pieces)
+    ]
+    for copy in ins:
+        copy.start()
+    for into, out in zip(ins, outs):
+        into.wait()
+        out.start()
+    for copy in outs:
+        copy.wait()
+
+
+def pack(x):
+    return pl.pallas_call(
+        pack_kernel,
+        out_shape=jax.ShapeDtypeStruct((2, 64, 8, 128), jnp.float32),
+        in_specs=[pl.BlockSpec(memory_space=pltpu.HBM)],
+        out_specs=pl.BlockSpec(memory_space=pltpu.HBM),
+        scratch_shapes=[pltpu.VMEM((2, 64, 8, 128), jnp.float32), pltpu.SemaphoreType.DMA((2, 8))],
+        compiler_params=pltpu.CompilerParams(vmem_limit_bytes=66_300_000),
+        cost_estimate=pl.CostEstimate(flops=1 << 18, bytes_accessed=1 << 20, transcendentals=0),
+        name="pack",
+    )(x.reshape(64, 2, 8, 128))
+
+
 def weigh_kernel(g_ref, w_ref, re_ref, im_ref, turned, real, imag, sems):
     weights = w_ref[...]
     copies = []
@@ -200,7 +231,7 @@
 
 def per_device(grid_field, lat_weight):
     table = stage(jnp.asarray(mode_tables()))
-    x = grid_field.reshape(64, 2, 8, 128)[:, ::-1].transpose(1, 0, 2, 3).reshape(32, 32, 128)
+    x = pack(grid_field).reshape(32, 32, 128)
     y = lax.all_to_all(x, ("far", "lon"), 0, 0, tiled=True, axis_index_groups=first())
     z = transform(y, table)
     g = lax.all_to_all(z.reshape(128, 8, 128), ("near", "lon"), 0, 0, tiled=True, axis_index_groups=second())

time: 55.9 us -> 55.9 us (level)
  local copies, waits for them, and re-layouts: 3.5 us -> 1.59 us
  Pallas kernels: 1.84 us -> 3.69 us
    pallas_call x0 -> x1, Pallas kernels: none -> 1.84 us  [pack(): pl.pallas_call(pack_kernel, out_shape=jax.ShapeDtypeStruct((2, 64, 8, 128...]
    reshape x1 -> x0, local copies, waits for them, and re-layouts: 1.08 us -> none  [per_device(): grid_field.reshape(64, 2, 8, 128)[:, ::-1].transpose(1, 0, 2, 3)]
    rev x1 -> x0, local copies, waits for them, and re-layouts: 0.83 us -> none  [per_device(): grid_field.reshape(64, 2, 8, 128)[:, ::-1].transpose(1, 0, 2, 3)]
where the time goes in v7:
time: 55.9 us; the launch traced here: 55.6 us
  blocking collectives  25.9 us (46%)
  starting transfers between devices  13.9 us (25%)
  waiting for transfers between devices  9.78 us (17%)
  Pallas kernels  3.69 us (7%)
  local copies, waits for them, and re-layouts  1.59 us (3%)
  between operations  0.68 us (1%)
    all_to_all x1, blocking collectives, per_device(): lax.all_to_all(z.reshape(128, 8, 128), ('near', 'lon'), 0, 0, tiled=True,...  25.9 us
    all_to_all x1, starting transfers between devices, per_device(): lax.all_to_all(x, ('far', 'lon'), 0, 0, tiled=True, axis_index_groups=fir...  13.9 us
    all_to_all x1, waiting for transfers between devices, per_device(): lax.all_to_all(x, ('far', 'lon'), 0, 0, tiled=True, axis_index_groups=fir...  9.78 us
    pallas_call x1, Pallas kernels, pack(): pl.pallas_call(pack_kernel, out_shape=jax.ShapeDtypeStruct((2, 64, 8, 128...  1.84 us
    unnamed x4, local copies, waits for them, and re-layouts  1.59 us
  transfers between devices with their start and end apart: 1, of which 1 were waited for; matrix products, arithmetic and copies ran while one was open for 0% of the time, Pallas kernels for 0%

profile of v7, /device:TPU:1, one launch (start us, length us, event | category | flops | bytes accessed | tf_op | source)
XLA Modules:
  0.0 55.6 jit_solution(7688920765305667226)
XLA Ops:
  0.6 1.8 %pack.1 = f32[2,64,8,128]{3,2,1,0:T(8,128)} custom-call(f32[64,2,8,128]{3,2,1,0:T(8,128)} %bitcast.19), custom_call_target="tpu_custom_call" | custom-call | flops 262144 | bytes 1048576 | tf_op jit(solution)/shard_map/pack/pallas_call | solution.py:181
  2.5 13.9 %all-to-all-start = ((f32[32,32,128]{2,1,0:T(8,128)}), f32[32,32,128]{2,1,0:T(8,128)S(1)}, u32[]{:S(2)}, u32[]{:S(2)}) async-start(f32[32,32,128]{2,1,0:T(8,128)} %bitcast.18), calls=%async_computation | async-start | bytes 1048576 | tf_op jit(solution)/shard_map/all_to_all | solution.py:235
  16.4 0.0 copy-start
  16.4 1.6 %copy-done = bf16[2,8,256,256]{3,2,1,0:T(8,128)(2,1)S(1)} copy-done((bf16[2,8,256,256]{3,2,1,0:T(8,128)(2,1)S(1)}, bf16[2,8,256,256]{3,2,1,0:T(8,128)(2,1)}, u32[]{:S(2)}) %copy-start) | copy-done | bytes 2097176
  18.0 0.1 stage.1.table_ref
  18.2 0.0 copy-start.1
  18.2 9.8 %all-to-all-done.y_ref = f32[32,32,128]{2,1,0:T(8,128)S(1)} async-done(((f32[32,32,128]{2,1,0:T(8,128)}), f32[32,32,128]{2,1,0:T(8,128)S(1)}, u32[]{:S(2)}, u32[]{:S(2)}) %all-to-all-start) | async-done | bytes 524320 | tf_op jit(solution)/shard_map/all_to_all | solution.py:235
  28.0 0.7 %transform.1 = f32[1024,128]{1,0:T(8,128)S(1)} custom-call(f32[32,32,128]{2,1,0:T(8,128)S(1)} %all-to-all-done.y_ref, bf16[2,8,256,256]{3,2,1,0:T(8,128)(2,1)S(1)} %stage.1.table_ref), custom_call_target="tpu_custom_call" | custom-call | flops 201326592 | bytes 3145728 | tf_op jit(solution)/shard_map/transform/pallas_call | solution.py:147
  28.7 25.9 %all_to_all.10 = f32[128,8,128]{2,1,0:T(8,128)S(1)} all-to-all(f32[128,8,128]{2,1,0:T(8,128)S(1)} %bitcast.16), channel_id=1, replica_groups={{197,198,199,192,193,194,195,196,69,70,71,64,65,66,67,68,213,214,215,20..., dimensions={0} | all-to-all | bytes 1048576 | tf_op jit(solution)/shard_map/all_to_all | solution.py:237
  54.6 0.0 copy-done.1
  54.6 1.0 %weigh.1 = (f32[4,64,256]{2,1,0:T(8,128)}, f32[4,64,256]{2,1,0:T(8,128)}) custom-call(f32[1024,128]{1,0:T(8,128)S(1)} %bitcast.15, f32[1,256]{1,0:T(1,128)S(1)} %bitcast.17), custom_call_target="tpu_custom_call" | custom-call | flops 262144 | bytes 1048576 | tf_op jit(solution)/shard_map/weigh/pallas_call | solution.py:215
Async XLA Ops:
  2.5 25.5 %all-to-all-start = ((f32[32,32,128]{2,1,0:T(8,128)}), f32[32,32,128]{2,1,0:T(8,128)S(1)}, u32[]{:S(2)}, u32[]{:S(2)}) async-start(f32[32,32,128]{2,1,0:T(8,128)} %bitcast.18), calls=%async_computation | async-start | bytes 1048576 | tf_op jit(solution)/shard_map/all_to_all | solution.py:235
  16.4 1.6 %copy-start = (bf16[2,8,256,256]{3,2,1,0:T(8,128)(2,1)S(1)}, bf16[2,8,256,256]{3,2,1,0:T(8,128)(2,1)}, u32[]{:S(2)}) copy-start(bf16[2,8,256,256]{3,2,1,0:T(8,128)(2,1)} %constant.2.clone.table_ref) | copy-start | bytes 6291460
  18.2 36.5 %copy-start.1 = (f32[256]{0:T(256)S(1)}, f32[256]{0:T(256)}, u32[]{:S(2)}) copy-start(f32[256]{0:T(256)} %param.4) | copy-start | bytes 3076
